TPU v7x, 32 devices: a whole 2x2x4 slice. The times are simulated.
32 devices in a mesh: coil: 8 (over y, x, core), kz: 4 (over z).
Axes of the slice: x: 2, y: 2, z: 4, core: 2. Of those that a mesh axis runs over, the one named last changes fastest.
Arguments:
- kdata: bfloat16 [2, 64, 8, 256, 512], P(None, 'kz', 'coil'), may hold values from -6 to 6
- spoke_angle: int32 [256], replicated, may hold values from 0 to 63
- spoke_count: int32 [64], P('kz'), may hold values from 128 to 256
- block_index: int32 [64, 4], replicated, may hold values from 0 to 511
- interp: bfloat16 [64, 4, 128, 128], replicated, may hold values from -0.5 to 0.5
- sens_maps: bfloat16 [2, 8, 256, 256], P(None, 'coil'), may hold values from -5 to 5
Outputs:
- image: float32 [2, 64, 256, 256], P(None, 'kz', 'coil')
Inputs may be any that keep to these rules, and one draw needn't show every extreme that they name: Partition p uses its first spoke_count[p] spokes. `block_index`: several segments may hit the same grid block.
All inputs are finite; a program needn't handle non-finite values.
Results may differ from a plain program's by a relative error of at most 0.0059.
Values sent between devices are 32-bit elements; how exact they have to be, the bound alone decides.
No kernel may reach another device: no remote copies, remote signals or barrier semaphores. Data moves between devices by JAX's collectives and lax.ppermute only.
A program may use at most 128 MiB of HBM per device.

v0:
```python
import jax
import jax.numpy as jnp
from jax import lax
from jax.sharding import PartitionSpec as P


def dft_tables(length, dtype):
    index = jnp.arange(length, dtype=jnp.int32)
    product = index[:, None] * index[None, :] % length
    phase = product.astype(jnp.float32) * (2.0 * jnp.pi / length)
    scale = 1.0 / jnp.sqrt(jnp.float32(length))
    return ((jnp.cos(phase) * scale).astype(dtype), (jnp.sin(phase) * scale).astype(dtype))


def kz_block(z_first, z_count, k_count, length):
    z_index = z_first + jnp.arange(z_count, dtype=jnp.int32)
    k_index = jnp.arange(k_count, dtype=jnp.int32)
    product = z_index[:, None] * k_index[None, :] % length
    phase = product.astype(jnp.float32) * (2.0 * jnp.pi / length)
    scale = 1.0 / jnp.sqrt(jnp.float32(length))
    return (jnp.cos(phase) * scale, jnp.sin(phase) * scale)


def kz_apply(cos_z, sin_z, slab):
    high = lax.Precision.HIGHEST
    real_part = jnp.einsum("zk,kyx->zyx", cos_z, slab[0], precision=high) + jnp.einsum(
        "zk,kyx->zyx", sin_z, slab[1], precision=high
    )
    imag_part = jnp.einsum("zk,kyx->zyx", cos_z, slab[1], precision=high) - jnp.einsum(
        "zk,kyx->zyx", sin_z, slab[0], precision=high
    )
    return jnp.stack([real_part, imag_part])


def coil_image(data, weights, interp, block_index, cos_t, sin_t):
    f32 = jnp.float32
    binned = jnp.einsum("rpsn,psa->rpan", data, weights, preferred_element_type=f32).astype(
        jnp.bfloat16
    )
    rdim, pdim, adim, mdim = binned.shape
    seg = interp.shape[2]
    gdim = mdim // seg
    side = cos_t.shape[0]
    pieces = binned.reshape(rdim, pdim, adim, gdim, seg)
    contrib = jnp.einsum("rpagj,agjt->rpagt", pieces, interp, preferred_element_type=f32)
    flat = jnp.zeros((rdim, pdim, side * side // seg, seg), f32)
    flat = flat.at[:, :, block_index.reshape(-1)].add(contrib.reshape(rdim, pdim, adim * gdim, seg))
    grid = flat.reshape(rdim, pdim, side, side).astype(jnp.bfloat16)
    half_re = jnp.einsum("ky,pyx->pkx", cos_t, grid[0], preferred_element_type=f32) + jnp.einsum(
        "ky,pyx->pkx", sin_t, grid[1], preferred_element_type=f32
    )
    half_im = jnp.einsum("ky,pyx->pkx", cos_t, grid[1], preferred_element_type=f32) - jnp.einsum(
        "ky,pyx->pkx", sin_t, grid[0], preferred_element_type=f32
    )
    half_re = half_re.astype(jnp.bfloat16)
    half_im = half_im.astype(jnp.bfloat16)
    out_re = jnp.einsum("pkx,mx->pkm", half_re, cos_t, preferred_element_type=f32) + jnp.einsum(
        "pkx,mx->pkm", half_im, sin_t, preferred_element_type=f32
    )
    out_im = jnp.einsum("pkx,mx->pkm", half_im, cos_t, preferred_element_type=f32) - jnp.einsum(
        "pkx,mx->pkm", half_re, sin_t, preferred_element_type=f32
    )
    return jnp.stack([out_re, out_im])


def conj_product(sens, image):
    real_part = sens[0] * image[0] + sens[1] * image[1]
    imag_part = sens[0] * image[1] - sens[1] * image[0]
    return jnp.stack([real_part, imag_part])


def per_device(kdata, spoke_angle, spoke_count, block_index, interp, sens_maps):
    side = sens_maps.shape[2]
    parts_here = kdata.shape[1]
    spokes = kdata.shape[3]
    angles = interp.shape[0]
    cos_t, sin_t = dft_tables(side, jnp.bfloat16)
    position = jnp.arange(spokes, dtype=jnp.int32)
    used = position[None, :] < spoke_count[:, None]
    match = spoke_angle[:, None] == jnp.arange(angles, dtype=jnp.int32)[None, :]
    weights = (used[:, :, None] & match[None, :, :]).astype(jnp.bfloat16)
    data = kdata[:, :, 0]
    image_c = coil_image(data, weights, interp, block_index, cos_t, sin_t)
    sens_here = sens_maps.astype(jnp.float32)
    weighted = conj_product(sens_here[:, 0][:, None], image_c)
    combined = lax.psum_scatter(weighted, "coil", scatter_dimension=2, tiled=True)
    groups = lax.axis_size("kz")
    kz_total = parts_here * groups
    my_first = lax.axis_index("kz") * parts_here
    piece = lax.all_gather(combined, "kz", axis=1, tiled=True)
    cos_z, sin_z = kz_block(my_first, parts_here, piece.shape[1], kz_total)
    return kz_apply(cos_z, sin_z, piece)


def solution(mesh):
    placed = (
        P(None, "kz", "coil", None, None),
        P(),
        P("kz"),
        P(),
        P(),
        P(None, "coil", None, None),
    )
    return jax.shard_map(
        per_device,
        mesh=mesh,
        in_specs=placed,
        out_specs=P(None, "kz", "coil", None),
        check_vma=False,
    )
```

profile of v0, /device:TPU:0, one launch (start us, length us, event | category | flops | bytes accessed | tf_op | source)
XLA Modules:
  0.0 278.6 jit_solution(6729629359910109795)
XLA Ops:
  8.0 6.2 %convert_bitcast_fusion = bf16[2,16,64,512]{3,2,0,1:T(8,128)(2,1)} fusion(pred[256,64]{0,1:T(8,128)(4,1)S(1)} %iota_compare_fusion, pred[16,256]{1,0:T(8,128)(4,1)S(1)} %iota_compare_fusion.1, bf16[2,16,1,256,512]{4,3,2,1,0:T(8,128)(2,1)} %param.6), kind=kOutput, calls=%fused_computation.21 | convolution fusion | flops 538181632 | bytes 10506240 | tf_op jit(solution)/shard_map/rpsn,psa->rpan/dot_general | solution.py:37
  14.2 2.6 reshape.89
  17.0 7.7 %fusion = f32[64,4,2,16,128]{4,3,2,1,0:T(8,128)} fusion(bf16[64,4,128,128]{3,2,1,0:T(8,128)(2,1)} %param.10, bf16[2,16,64,4,128]{4,3,2,0,1:T(4,128)(2,1)S(1)} %reshape.89), kind=kOutput, calls=%fused_computation.2 | convolution fusion | flops 268435456 | bytes 14680064 | tf_op jit(solution)/shard_map/rpagj,agjt->rpagt/dot_general | solution.py:45
  24.6 3.8 %broadcast_in_dim.2 = f32[2,16,512,128]{3,1,2,0:T(8,128)} broadcast(f32[]{:T(128)} %constant.42.clone.1), dimensions={} | broadcast | bytes 8388612 | tf_op jit(solution)/shard_map/broadcast_in_dim | solution.py:46
  28.4 34.6 %scatter_fusion = f32[2,16,512,128]{3,1,2,0:T(8,128)} fusion(f32[2,16,512,128]{3,1,2,0:T(8,128)} %broadcast_in_dim.2, s32[256]{0:T(256)S(1)} %bitcast.87, f32[256,2,16,128]{3,2,1,0:T(8,128)} %bitcast.86), kind=kCustom, calls=%fused_computation | custom fusion | flops 1048576 | bytes 12583936 | tf_op jit(solution)/shard_map/scatter-add | solution.py:47
  63.0 3.9 %convert_element_type.68 = bf16[2,16,512,128]{3,1,2,0:T(8,128)(2,1)S(1)} convert(f32[2,16,512,128]{3,1,2,0:T(8,128)} %scatter_fusion) | non-fusion elementwise | flops 2097152 | bytes 12582912 | tf_op jit(solution)/shard_map/convert_element_type | solution.py:48
  66.9 2.0 fusion.133
  69.0 1.9 copy.21
  70.9 2.7 squeeze.11
  73.6 3.6 %fusion.53 = f32[16,256,256]{2,1,0:T(8,128)} fusion(bf16[16,256,256]{2,1,0:T(8,128)(2,1)S(1)} %squeeze.11), kind=kOutput, calls=%fused_computation.55 | convolution fusion | flops 537919488 | bytes 6291456 | tf_op jit(solution)/shard_map/ky,pyx->pkx/dot_general | solution.py:49
  77.2 1.9 copy.23
  79.0 4.1 %squeeze.12 = bf16[16,256,256]{2,1,0:T(8,128)(2,1)} reshape(bf16[1,16,512,128]{3,2,1,0:T(8,128)(2,1)} %copy.23) | data formatting | bytes 4194304 | tf_op jit(solution)/shard_map/squeeze | solution.py:50
  83.2 3.4 %fusion.50 = f32[16,256,256]{2,1,0:T(8,128)S(1)} fusion(bf16[16,256,256]{2,1,0:T(8,128)(2,1)} %squeeze.12), kind=kOutput, calls=%fused_computation.54 | convolution fusion | flops 537919488 | bytes 6291456 | tf_op jit(solution)/shard_map/ky,pyx->pkx/dot_general | solution.py:52
  86.6 1.7 add_convert_fusion
  88.3 1.7 subtract_convert_fusion
  95.2 2.7 add_bitcast_fusion
  97.9 3.8 %pad_maximum_fusion = f32[2,16,256,256]{3,2,1,0:T(8,128)} fusion(f32[1,16,256,256]{3,2,1,0:T(8,128)S(1)} %get-tuple-element.6, f32[1,16,256,256]{3,2,1,0:T(8,128)S(1)} %get-tuple-element.5), kind=kLoop, calls=%fused_computation.1 | loop fusion | flops 2097152 | bytes 16777216 | tf_op jit(solution)/shard_map/stack | solution.py:69
  101.8 74.3 %reduce-scatter.2.cloned.1.call-done = f32[2,16,32,256]{3,2,1,0:T(8,128)} async-done(((f32[2,16,256,256]{3,2,1,0:T(8,128)}), f32[2,16,32,256]{3,2,1,0:T(8,128)}) %reduce-scatter.2.cloned.1.call-update) | async-done | bytes 1048592 | tf_op jit(solution)/shard_map/reduce_scatter | solution.py:86
  176.1 82.3 %all-gather.2.cloned.1.call-done = f32[2,64,32,256]{3,2,1,0:T(8,128)} async-done(((f32[2,16,32,256]{3,2,1,0:T(8,128)}), f32[2,64,32,256]{3,2,1,0:T(8,128)}) %all-gather.2.cloned.1.call-update) | async-done | bytes 4194320 | tf_op jit(solution)/shard_map/all_gather | solution.py:90
  258.3 2.5 slice_bitcast_fusion.1
  260.9 2.3 fusion.13
  263.2 2.3 fusion.11
  265.5 2.3 fusion.24
  267.8 2.3 fusion.30
  (27 shorter events, 8.5 us)
Async XLA Ops:
  6.5 169.5 %reduce-scatter.2.cloned.1.call-start = ((), (), s32[]{:S(2)}) async-start(), calls=%async_computation.1 | async-start | bytes 9437184 | tf_op jit(solution)/shard_map/reduce_scatter | solution.py:86
  14.2 2.6 copy-start.4
  73.5 3.6 %copy-start.2 = (bf16[1,16,512,128]{3,1,2,0:T(8,128)(2,1)S(1)}, bf16[1,16,512,128]{3,1,2,0:T(8,128)(2,1)}, u32[]{:S(2)}) copy-start(bf16[1,16,512,128]{3,1,2,0:T(8,128)(2,1)} %get-tuple-element.9) | copy-start | bytes 6291460
  83.2 3.4 %copy-start = (bf16[16,256,256]{2,1,0:T(8,128)(2,1)S(1)}, bf16[16,256,256]{2,1,0:T(8,128)(2,1)}, u32[]{:S(2)}) copy-start(bf16[16,256,256]{2,1,0:T(8,128)(2,1)} %squeeze.12) | copy-start | bytes 6291460
  83.2 3.5 %copy-start.1 = (f32[16,256,256]{2,1,0:T(8,128)S(1)}, f32[16,256,256]{2,1,0:T(8,128)}, u32[]{:S(2)}) copy-start(f32[16,256,256]{2,1,0:T(8,128)} %fusion.53) | copy-start | bytes 12582916
  93.4 1.7 copy-start.3
  101.7 156.6 %all-gather.2.cloned.1.call-start = ((), (), s32[]{:S(2)}) async-start(), calls=%async_computation.2 | async-start | bytes 5242880 | tf_op jit(solution)/shard_map/all_gather | solution.py:90
Sparse Core Ops, SparseCore 0:
  101.8 74.1 reduce-scatter.1
  177.6 80.7 all-gather.1
where the time goes:
time: 279 us
  waiting for transfers between devices  157 us (56%)
  other arithmetic  43.9 us (16%)
  matrix products  41.2 us (15%)
  local copies, waits for them, and re-layouts  23.3 us (8%)
  between operations  13.6 us (5%)
    all_gather x1, waiting for transfers between devices, per_device(): piece = lax.all_gather(combined, 'kz', axis=1, tiled=True)  82.3 us
    reduce_scatter x1, waiting for transfers between devices, per_device(): lax.psum_scatter(weighted, 'coil', scatter_dimension=2, tiled=True)  74.3 us
    scatter-add x1, other arithmetic, coil_image(): flat.at[:, :, block_index.reshape(-1)]  34.6 us
    dot_general x1, matrix products, coil_image(): jnp.einsum('rpagj,agjt->rpagt', pieces, interp, preferred_element_type=f32)  7.66 us
    dot_general x1, matrix products, coil_image(): jnp.einsum('rpsn,psa->rpan', data, weights, preferred_element_type=f32)  6.2 us
  transfers between devices with their start and end apart: 2, of which 2 were waited for; matrix products, arithmetic and copies ran while one was open for 0% of the time, Pallas kernels for 0%

commit v1 on v0

--- a/solution.py
+++ b/solution.py
@@ -1,7 +1,291 @@
 import jax
 import jax.numpy as jnp
+import numpy as np
 from jax import lax
+from jax.experimental import pallas as pl
+from jax.experimental.pallas import tpu as pltpu
 from jax.sharding import PartitionSpec as P
+
+
+def host_tables(length, dtype):
+    index = np.arange(length, dtype=np.int32)
+    product = index[:, None] * index[None, :] % length
+    phase = product.astype(np.float32) * np.float32(2.0 * np.pi / length)
+    scale = np.float32(1.0) / np.sqrt(np.float32(length))
+    return ((np.cos(phase) * scale).astype(dtype), (np.sin(phase) * scale).astype(dtype))
+
+
+def grid_kernel(
+    count_ref, bidx_ref, rows_ref, angle_ref, cos_ref, sin_ref, sens_ref, data_ref, interp_hbm,
+    half_ref, sensp_ref,
+    bin_ref, grid_ref, m1_ref, interp_ref, sem,
+):
+    f32, bf16 = jnp.float32, jnp.bfloat16
+    step = pl.program_id(0)
+    parts = pl.num_programs(0) // 2
+    angles, segs = bidx_ref.shape
+    seg = interp_ref.shape[1]
+    side = cos_ref.shape[0]
+    spokes = angle_ref.shape[1]
+    lines = 2 * bin_ref.shape[1] // (2 * angles)
+    nblocks = grid_ref.shape[0] // lines
+    per_row = side // seg
+    nparts = lines // 2
+
+    @pl.when(step == 0)
+    def _():
+        pltpu.make_async_copy(interp_hbm, interp_ref, sem).start()
+        pick = (lax.broadcasted_iota(jnp.int32, (side, side), 1) == rows_ref[...]).astype(bf16)
+        pc = jnp.dot(pick, cos_ref[...], preferred_element_type=f32)
+        ps = jnp.dot(pick, sin_ref[...], preferred_element_type=f32)
+        m1_ref[:side, :side] = pc.astype(bf16)
+        m1_ref[:side, side:] = ps.astype(bf16)
+        m1_ref[side:, :side] = (-ps).astype(bf16)
+        m1_ref[side:, side:] = pc.astype(bf16)
+        for r in range(2):
+            sensp_ref[r] = jnp.dot(pick, sens_ref[r], preferred_element_type=f32)
+
+    @pl.when(step < parts)
+    def _():
+        zrows = grid_ref.shape[0] // nparts
+        grid_ref[pl.ds(step * zrows, zrows), :] = jnp.zeros((zrows, seg), f32)
+        a_iota = lax.broadcasted_iota(jnp.int32, (angles, spokes), 0)
+        s_iota = lax.broadcasted_iota(jnp.int32, (angles, spokes), 1)
+        keep = (a_iota == angle_ref[...]) & (s_iota < count_ref[step])
+        wt = jnp.where(keep, 1.0, 0.0).astype(bf16)
+        for r in range(2):
+            b = jnp.dot(wt, data_ref[r, 0], preferred_element_type=f32)
+            b = b.astype(bf16).astype(f32)
+            for g in range(segs):
+                bin_ref[g, pl.ds((r * nparts + step) * angles, angles), :] = b[:, g * seg:(g + 1) * seg]
+
+    @pl.when(step == parts)
+    def _():
+        pltpu.make_async_copy(interp_hbm, interp_ref, sem).wait()
+        unroll = 4 if angles % 4 == 0 else 1
+
+        def body(i, carry):
+            res = []
+            for u in range(unroll):
+                a = i * unroll + u
+                for g in range(segs):
+                    lhs = bin_ref[g, pl.ds(a, lines, stride=angles), :].astype(bf16)
+                    res.append((bidx_ref[a, g], jnp.dot(lhs, interp_ref[a * segs + g], preferred_element_type=f32)))
+            for b, v in res:
+                at = pl.ds(pl.multiple_of(b * lines, lines), lines)
+                grid_ref[at, :] = grid_ref[at, :] + v
+            return carry
+
+        lax.fori_loop(0, angles // unroll, body, 0)
+
+    @pl.when(step >= parts)
+    def _():
+        p = step - parts
+        stacked = jnp.concatenate(
+            [
+                jnp.concatenate(
+                    [
+                        grid_ref[pl.ds(h * lines + r * nparts + p, side, stride=per_row * lines), :].astype(bf16)
+                        for h in range(per_row)
+                    ],
+                    axis=1,
+                )
+                for r in range(2)
+            ],
+            axis=0,
+        )
+        half = jnp.dot(m1_ref[...], stacked, preferred_element_type=f32).astype(bf16)
+        half_ref[0, :, :side] = half[:side]
+        half_ref[0, :, side:] = half[side:]
+
+
+def image_kernel(half_ref, m2_ref, sens_ref, send_ref, keep_ref):
+    pp, side, depth = half_ref.shape
+    width = m2_ref.shape[1] // 2
+    pieces = keep_ref.shape[0]
+    sub = keep_ref.shape[3]
+    out = jnp.dot(half_ref[...].reshape(pp * side, depth), m2_ref[...], preferred_element_type=jnp.float32)
+    for q in range(pp):
+        re = out[q * side:(q + 1) * side, :width]
+        im = out[q * side:(q + 1) * side, width:]
+        w = (sens_ref[0] * re + sens_ref[1] * im, sens_ref[0] * im - sens_ref[1] * re)
+        for r in range(2):
+            keep_ref[:, r, q] = w[r][:side // 2].reshape(pieces, sub, width)
+            send_ref[:, r, q] = w[r][side // 2:].reshape(pieces, sub, width)
+
+
+def kz_kernel(z_ref, *refs):
+    n = len(refs) // 2
+    ins, outs = refs[:n], refs[n:]
+    rows, width = ins[0].shape
+    sub = 8
+    cnt = rows // (2 * sub)
+    x = jnp.concatenate(
+        [
+            jnp.concatenate(
+                [ins[s][pl.ds(r * cnt * sub + i, cnt, stride=sub), :] for s in range(n) for r in range(2)], axis=0
+            )
+            for i in range(sub)
+        ],
+        axis=1,
+    )
+    y = jnp.dot(z_ref[...], x, preferred_element_type=jnp.float32, precision=lax.Precision.HIGHEST)
+    for s in range(n):
+        for r in range(2):
+            for i in range(sub):
+                outs[s][pl.ds(r * cnt * sub + i, cnt, stride=sub), :] = y[
+                    (s * 2 + r) * cnt:(s * 2 + r + 1) * cnt, i * width:(i + 1) * width
+                ]
+
+
+def place_kernel(me_ref, *refs):
+    out_ref = refs[-1]
+    ins = refs[:-1]
+    n = out_ref.shape[2] // ins[0].shape[2]
+    width = ins[0].shape[3]
+    sub = ins[0].shape[2]
+    for j in range(len(ins) // n):
+        for s in range(n):
+            at = pl.multiple_of((me_ref[0] ^ s) * sub, sub)
+            out_ref[:, :, pl.ds(at, sub), j * width:(j + 1) * width] = ins[j * n + s][...]
+
+
+def swap(x, axis, bit):
+    n = lax.axis_size(axis)
+    return lax.ppermute(x, axis, [(i, i ^ bit) for i in range(n)])
+
+
+def piece_order():
+    order = []
+    for relc in range(2):
+        order += [(relc, 1, ry, rd) for ry in range(2) for rd in (0, 1)]
+        order += [(relc, 0, ry, rd) for ry in range(2) for rd in (0, 1)]
+        order += [(relc, rx, 1, rd) for rx in range(2) for rd in (2, 3)]
+        order += [(relc, rx, 0, rd) for rx in range(2) for rd in (2, 3)]
+    coil_rel = np.array([c + 2 * x + 4 * y for c, x, y, d in order], np.int32)
+    kz_rel = np.array([d for c, x, y, d in order], np.int32)
+    return coil_rel, kz_rel
+
+
+def fast_device(kdata, spoke_angle, spoke_count, block_index, interp, sens_maps):
+    f32, bf16 = jnp.float32, jnp.bfloat16
+    _, parts, _, spokes, samples = kdata.shape
+    side = sens_maps.shape[2]
+    angles, segs, seg, _ = interp.shape
+    groups = lax.axis_size("kz")
+    mine_c = lax.axis_index("coil")
+    mine_d = lax.axis_index("kz")
+    sub = side // (lax.axis_size("coil") * groups)
+    coil_rel, kz_rel = piece_order()
+    starts = (mine_c ^ coil_rel) * (sub * groups) + (mine_d ^ kz_rel) * sub
+    rows = (starts[:, None] + np.arange(sub, dtype=np.int32)[None, :]).reshape(side, 1)
+    cos_h, sin_h = host_tables(side, np.float32)
+    cos_t, sin_t = jnp.asarray(cos_h).astype(bf16), jnp.asarray(sin_h).astype(bf16)
+    lines = 2 * parts
+    smem = pl.BlockSpec(memory_space=pltpu.SMEM)
+    whole = lambda shape: pl.BlockSpec(shape, lambda i: (0,) * len(shape))
+    half, sens_p = pl.pallas_call(
+        grid_kernel,
+        grid=(2 * parts,),
+        in_specs=[
+            smem, smem, whole((side, 1)), whole((1, spokes)), whole((side, side)), whole((side, side)),
+            whole((2, side, side)),
+            pl.BlockSpec((2, 1, spokes, samples), lambda i: (0, jnp.minimum(i, parts - 1), 0, 0)),
+            pl.BlockSpec(memory_space=pl.ANY),
+        ],
+        out_specs=[
+            pl.BlockSpec((1, side, 2 * side), lambda i: (jnp.maximum(i - parts, 0), 0, 0)),
+            whole((2, side, side)),
+        ],
+        out_shape=[
+            jax.ShapeDtypeStruct((parts, side, 2 * side), bf16),
+            jax.ShapeDtypeStruct((2, side, side), f32),
+        ],
+        scratch_shapes=[
+            pltpu.VMEM((segs, lines * angles, seg), f32),
+            pltpu.VMEM((side * side // seg * lines, seg), f32),
+            pltpu.VMEM((2 * side, 2 * side), bf16),
+            pltpu.VMEM((angles * segs, seg, seg), bf16),
+            pltpu.SemaphoreType.DMA,
+        ],
+        compiler_params=pltpu.CompilerParams(
+            dimension_semantics=("arbitrary",), vmem_limit_bytes=48 * 1024 * 1024
+        ),
+        name="grid_half",
+    )(
+        spoke_count, block_index, rows, spoke_angle.reshape(1, spokes), cos_t, sin_t,
+        sens_maps[:, 0], kdata[:, :, 0], interp.reshape(angles * segs, seg, seg),
+    )
+
+    width = 128
+    chunks = side // width
+    pp = 4
+    npieces = len(coil_rel) // 2
+    piece = (2, parts, sub, width)
+    kz_total = parts * groups
+    order = ((mine_d ^ np.arange(groups, dtype=np.int32))[:, None] * parts + np.arange(parts, dtype=np.int32)[None, :])
+    prod = order[:, None, :, None] * order[None, :, None, :] % kz_total
+    phase = prod.astype(f32) * (2.0 * jnp.pi / kz_total)
+    scale = 1.0 / jnp.sqrt(f32(kz_total))
+    cz, sz = jnp.cos(phase) * scale, jnp.sin(phase) * scale
+    zmat = jnp.stack([jnp.stack([cz, sz], 3), jnp.stack([-sz, cz], 3)], 1)
+    zmat = jnp.transpose(zmat, (0, 1, 3, 2, 4, 5)).reshape(2 * kz_total, 2 * kz_total)
+
+    finals = []
+    for j in range(chunks):
+        cols = slice(j * width, (j + 1) * width)
+        ct, st = cos_h.T[:, cols], sin_h.T[:, cols]
+        m2 = np.concatenate([np.concatenate([ct, -st], 1), np.concatenate([st, ct], 1)], 0)
+        m2 = jnp.asarray(m2).astype(bf16)
+        out_spec = pl.BlockSpec((npieces, 2, pp, sub, width), lambda i: (0, 0, i, 0, 0))
+        out_type = jax.ShapeDtypeStruct((npieces,) + piece, f32)
+        send, keep = pl.pallas_call(
+            image_kernel,
+            grid=(parts // pp,),
+            in_specs=[
+                pl.BlockSpec((pp, side, 2 * side), lambda i: (i, 0, 0)),
+                pl.BlockSpec((2 * side, 2 * width), lambda i: (0, 0)),
+                pl.BlockSpec((2, side, width), lambda i, j=j: (0, 0, j)),
+            ],
+            out_specs=[out_spec, out_spec],
+            out_shape=[out_type, out_type],
+            compiler_params=pltpu.CompilerParams(
+                dimension_semantics=("arbitrary",), vmem_limit_bytes=48 * 1024 * 1024
+            ),
+            name="image_piece",
+        )(half, m2, sens_p)
+        got = swap(send, "coil", 1)
+        q = npieces // 4
+        h = q // 2
+        x_send = keep[:q] + got[:q]
+        y_send = keep[2 * q:3 * q] + got[2 * q:3 * q]
+        x_got = swap(x_send, "coil", 2)
+        y_got = swap(y_send, "coil", 4)
+        x_keep = keep[q:2 * q] + got[q:2 * q]
+        y_keep = keep[3 * q:] + got[3 * q:]
+        xy_send = x_keep[h:] + x_got[h:]
+        yx_send = y_keep[h:] + y_got[h:]
+        xy_got = swap(xy_send, "coil", 4)
+        yx_got = swap(yx_send, "coil", 2)
+        mine = [x_keep[s] + x_got[s] + xy_got[s] for s in range(h)]
+        mine += [y_keep[s] + y_got[s] + yx_got[s] for s in range(h)]
+        arrived = [mine[0]] + [swap(mine[s], "kz", s) for s in range(1, groups)]
+        flat = 2 * parts * sub
+        spun = pl.pallas_call(
+            kz_kernel,
+            out_shape=[jax.ShapeDtypeStruct((flat, width), f32)] * groups,
+            name="kz_dft",
+        )(zmat, *[v.reshape(flat, width) for v in arrived])
+        spun = [v.reshape(piece) for v in spun]
+        finals += [spun[0]] + [swap(spun[s], "kz", s) for s in range(1, groups)]
+    vm = pl.BlockSpec(memory_space=pltpu.VMEM)
+    return pl.pallas_call(
+        place_kernel,
+        in_specs=[smem] + [vm] * len(finals),
+        out_specs=vm,
+        out_shape=jax.ShapeDtypeStruct((2, parts, sub * groups, side), f32),
+        name="place",
+    )(mine_d.reshape(1).astype(jnp.int32), *finals)
 
 
 def dft_tables(length, dtype):
@@ -101,8 +385,9 @@
         P(),
         P(None, "coil", None, None),
     )
+    fast = mesh.shape["coil"] == 8 and mesh.shape["kz"] == 4
     return jax.shard_map(
-        per_device,
+        fast_device if fast else per_device,
         mesh=mesh,
         in_specs=placed,
         out_specs=P(None, "kz", "coil", None),

time: 279 us -> 133 us (0.48)
  waiting for transfers between devices: 157 us -> 38.3 us
  Pallas kernels: 0 us -> 44.3 us
  matrix products: 41.2 us -> 0 us
  other arithmetic: 43.9 us -> 3.79 us
  starting transfers between devices: 0.04 us -> 35.4 us
  between operations: 13.6 us -> 0.21 us
  local copies, waits for them, and re-layouts: 23.3 us -> 10.5 us
    all_gather x1 -> x0, waiting for transfers between devices: 82.3 us -> none  [per_device(): piece = lax.all_gather(combined, 'kz', axis=1, tiled=True)]
    reduce_scatter x1 -> x0, waiting for transfers between devices: 74.3 us -> none  [per_device(): lax.psum_scatter(weighted, 'coil', scatter_dimension=2, tiled=True)]
    pallas_call x0 -> x6, Pallas kernels: none -> 44.3 us  [the longest x1 28.6 us: fast_device(): pl.pallas_call(grid_kernel, grid=(2 * parts,), in_specs=[smem, smem, whol...]
    dot_general x14 -> x0, matrix products: 41.2 us -> none  [the longest x1 7.66 us: coil_image(): jnp.einsum('rpagj,agjt->rpagt', pieces, interp, preferred_element_type=f32)]
    ppermute x0 -> x22, waiting for transfers between devices: none -> 38.3 us  [swap(): return lax.ppermute(x, axis, [(i, i ^ bit) for i in range(n)])]
    ppermute x0 -> x22, starting transfers between devices: none -> 35.4 us  [swap(): return lax.ppermute(x, axis, [(i, i ^ bit) for i in range(n)])]
    scatter-add x1 -> x0, other arithmetic: 34.6 us -> none  [coil_image(): flat.at[:, :, block_index.reshape(-1)]]
    squeeze x3 -> x0, local copies, waits for them, and re-layouts: 9.34 us -> none  [the longest x1 4.13 us: coil_image(): grid[1]]
  transfers between devices with their start and end apart: 2 -> 22, of which waited for: 2 -> 7; matrix products, arithmetic and copies ran while one was open for 0% -> 3% of each run, Pallas kernels for 0% -> 7%
where the time goes in v1:
time: 133 us
  Pallas kernels  44.3 us (33%)
  waiting for transfers between devices  38.3 us (29%)
  starting transfers between devices  35.4 us (27%)
  local copies, waits for them, and re-layouts  10.5 us (8%)
  other arithmetic  3.79 us (3%)
    ppermute x22, waiting for transfers between devices, swap(): return lax.ppermute(x, axis, [(i, i ^ bit) for i in range(n)])  38.3 us
    ppermute x22, starting transfers between devices, swap(): return lax.ppermute(x, axis, [(i, i ^ bit) for i in range(n)])  35.4 us
    pallas_call x1, Pallas kernels, fast_device(): pl.pallas_call(grid_kernel, grid=(2 * parts,), in_specs=[smem, smem, whol...  28.6 us
    unnamed x41, local copies, waits for them, and re-layouts  8.9 us
    pallas_call x2, Pallas kernels, fast_device(): pl.pallas_call(image_kernel, grid=(parts // pp,), in_specs=[pl.BlockSpec(...  8.19 us
    pallas_call x2, Pallas kernels, fast_device(): pl.pallas_call(kz_kernel, out_shape=[jax.ShapeDtypeStruct((flat, width),...  5.06 us
  transfers between devices with their start and end apart: 22, of which 7 were waited for; matrix products, arithmetic and copies ran while one was open for 3% of the time, Pallas kernels for 7%

profile of v1, /device:TPU:0, one launch (start us, length us, event | category | flops | bytes accessed | tf_op | source)
XLA Modules:
  0.0 132.5 jit_solution(7449483125691445289)
XLA Ops:
  5.7 28.6 %grid_half.1 = (bf16[16,256,512]{2,1,0:T(8,128)(2,1)S(1)}, f32[2,256,256]{2,1,0:T(8,128)S(1)}) custom-call(s32[16]{0:T(128)S(1)} %copy-done.7, s32[64,4]{1,0:T(8,128)S(1)} %copy.22.bidx_ref, s32[256,1]{1,0:T(8,128)S(1)} %add.239.rows_ref, s32[1,256]{1,0:T(1,128)S(1)} %bitcast.40, bf16[256,256]{1,0:T(8,128)(2,1)S(1)} %copy-done.4, ...), custom_call_target="tpu_custom_call" | custom-call | tf_op jit(solution)/shard_map/grid_half/pallas_call | solution.py:187
  34.4 2.0 %copy-done = bf16[16,256,512]{2,1,0:T(8,128)(2,1)} copy-done((bf16[16,256,512]{2,1,0:T(8,128)(2,1)}, bf16[16,256,512]{2,1,0:T(8,128)(2,1)S(1)}, u32[]{:S(2)}) %copy-start) | copy-done | bytes 4194328
  36.4 4.1 %image_piece.3 = (f32[16,2,16,8,128]{4,3,2,1,0:T(8,128)S(1)}, f32[16,2,16,8,128]{4,3,2,1,0:T(8,128)S(1)}) custom-call(bf16[16,256,512]{2,1,0:T(8,128)(2,1)} %copy-done, bf16[512,256]{1,0:T(8,128)(2,1)S(1)} %copy-done.2, f32[2,256,256]{2,1,0:T(8,128)S(1)} %get-tuple-element.20.sens_ref), custom_call_target="tpu_custom_call" | custom-call | tf_op jit(solution)/shard_map/image_piece/pallas_call | solution.py:242
  41.1 4.1 %image_piece.2 = (f32[16,2,16,8,128]{4,3,2,1,0:T(8,128)S(1)}, f32[16,2,16,8,128]{4,3,2,1,0:T(8,128)S(1)}) custom-call(bf16[16,256,512]{2,1,0:T(8,128)(2,1)} %copy-done, bf16[512,256]{1,0:T(8,128)(2,1)S(1)} %copy-done.1, f32[2,256,256]{2,1,0:T(8,128)S(1)} %get-tuple-element.20.sens_ref), custom_call_target="tpu_custom_call" | custom-call | tf_op jit(solution)/shard_map/image_piece/pallas_call | solution.py:242
  46.3 3.0 %collective-permute-start.15 = (f32[4,2,16,8,128]{4,3,2,1,0:T(8,128)S(1)}, f32[4,2,16,8,128]{4,3,2,1,0:T(8,128)S(1)}, u32[]{:S(2)}, u32[]{:S(2)}) collective-permute-start(f32[4,2,16,8,128]{4,3,2,1,0:T(8,128)S(1)} %get-tuple-element.34), channel_id=1, source_target_pairs={{0,16},{4,20},{8,24},{12,28},{16,0},{20,4},{24,8},{28,12},{1,17},{... | collective-permute-start | bytes 1572872 | tf_op jit(solution)/shard_map/ppermute | solution.py:155
  49.4 1.6 %collective-permute-start.12 = (f32[4,2,16,8,128]{4,3,2,1,0:T(8,128)S(1)}, f32[4,2,16,8,128]{4,3,2,1,0:T(8,128)S(1)}, u32[]{:S(2)}, u32[]{:S(2)}) collective-permute-start(f32[4,2,16,8,128]{4,3,2,1,0:T(8,128)S(1)} %get-tuple-element.35), channel_id=1, source_target_pairs={{0,8},{4,12},{8,0},{12,4},{16,24},{20,28},{24,16},{28,20},{1,9},{5... | collective-permute-start | bytes 1572872 | tf_op jit(solution)/shard_map/ppermute | solution.py:155
  52.4 1.6 %collective-permute-start.1 = (f32[4,2,16,8,128]{4,3,2,1,0:T(8,128)S(1)}, f32[4,2,16,8,128]{4,3,2,1,0:T(8,128)S(1)}, u32[]{:S(2)}, u32[]{:S(2)}) collective-permute-start(f32[4,2,16,8,128]{4,3,2,1,0:T(8,128)S(1)} %get-tuple-element.39), channel_id=1, source_target_pairs={{0,8},{4,12},{8,0},{12,4},{16,24},{20,28},{24,16},{28,20},{1,9},{5... | collective-permute-start | bytes 1572872 | tf_op jit(solution)/shard_map/ppermute | solution.py:155
  54.0 8.1 %collective-permute-done.15 = f32[4,2,16,8,128]{4,3,2,1,0:T(8,128)S(1)} collective-permute-done((f32[4,2,16,8,128]{4,3,2,1,0:T(8,128)S(1)}, f32[4,2,16,8,128]{4,3,2,1,0:T(8,128)S(1)}, u32[]{:S(2)}, u32[]{:S(2)}) %collective-permute-start.15) | collective-permute-done | bytes 524320 | tf_op jit(solution)/shard_map/ppermute | solution.py:155
  62.1 2.1 %collective-permute-start.16 = (f32[2,2,16,8,128]{4,3,2,1,0:T(8,128)S(1)}, f32[2,2,16,8,128]{4,3,2,1,0:T(8,128)S(1)}, u32[]{:S(2)}, u32[]{:S(2)}) collective-permute-start(f32[2,2,16,8,128]{4,3,2,1,0:T(8,128)S(1)} %slice_add_fusion.8), channel_id=1, source_target_pairs={{0,8},{4,12},{8,0},{12,4},{16,24},{20,28},{24,16},{28,20},{1,9},{5... | collective-permute-start | bytes 786440 | tf_op jit(solution)/shard_map/ppermute | solution.py:155
  65.8 7.5 %collective-permute-done.4 = f32[4,2,16,8,128]{4,3,2,1,0:T(8,128)S(1)} collective-permute-done((f32[4,2,16,8,128]{4,3,2,1,0:T(8,128)S(1)}, f32[4,2,16,8,128]{4,3,2,1,0:T(8,128)S(1)}, u32[]{:S(2)}, u32[]{:S(2)}) %collective-permute-start.4) | collective-permute-done | bytes 524320 | tf_op jit(solution)/shard_map/ppermute | solution.py:155
  73.4 2.1 %collective-permute-start.5 = (f32[2,2,16,8,128]{4,3,2,1,0:T(8,128)S(1)}, f32[2,2,16,8,128]{4,3,2,1,0:T(8,128)S(1)}, u32[]{:S(2)}, u32[]{:S(2)}) collective-permute-start(f32[2,2,16,8,128]{4,3,2,1,0:T(8,128)S(1)} %slice_add_fusion.10), channel_id=1, source_target_pairs={{0,8},{4,12},{8,0},{12,4},{16,24},{20,28},{24,16},{28,20},{1,9},{5... | collective-permute-start | bytes 786440 | tf_op jit(solution)/shard_map/ppermute | solution.py:155
  77.1 4.0 %collective-permute-done.16 = f32[2,2,16,8,128]{4,3,2,1,0:T(8,128)S(1)} collective-permute-done((f32[2,2,16,8,128]{4,3,2,1,0:T(8,128)S(1)}, f32[2,2,16,8,128]{4,3,2,1,0:T(8,128)S(1)}, u32[]{:S(2)}, u32[]{:S(2)}) %collective-permute-start.16) | collective-permute-done | bytes 262176 | tf_op jit(solution)/shard_map/ppermute | solution.py:155
  81.1 2.7 %collective-permute-start.17 = (f32[2,16,8,128]{3,2,1,0:T(8,128)S(1)}, f32[2,16,8,128]{3,2,1,0:T(8,128)S(1)}, u32[]{:S(2)}, u32[]{:S(2)}) collective-permute-start(f32[2,16,8,128]{3,2,1,0:T(8,128)S(1)} %get-tuple-element.42), channel_id=1, source_target_pairs={{0,2},{1,3},{2,0},{3,1},{4,6},{5,7},{6,4},{7,5},{8,10},{9,11},{10,... | collective-permute-start | bytes 393224 | tf_op jit(solution)/shard_map/ppermute | solution.py:155
  86.2 2.9 %collective-permute-start.6 = (f32[2,16,8,128]{3,2,1,0:T(8,128)S(1)}, f32[2,16,8,128]{3,2,1,0:T(8,128)S(1)}, u32[]{:S(2)}, u32[]{:S(2)}) collective-permute-start(f32[2,16,8,128]{3,2,1,0:T(8,128)S(1)} %get-tuple-element.46), channel_id=1, source_target_pairs={{0,2},{1,3},{2,0},{3,1},{4,6},{5,7},{6,4},{7,5},{8,10},{9,11},{10,... | collective-permute-start | bytes 393224 | tf_op jit(solution)/shard_map/ppermute | solution.py:155
  91.1 4.0 %collective-permute-done.17 = f32[2,16,8,128]{3,2,1,0:T(8,128)S(1)} collective-permute-done((f32[2,16,8,128]{3,2,1,0:T(8,128)S(1)}, f32[2,16,8,128]{3,2,1,0:T(8,128)S(1)}, u32[]{:S(2)}, u32[]{:S(2)}) %collective-permute-start.17) | collective-permute-done | bytes 131104 | tf_op jit(solution)/shard_map/ppermute | solution.py:155
  97.4 2.5 %kz_dft.3 = (f32[256,128]{1,0:T(8,128)}, f32[256,128]{1,0:T(8,128)}, f32[256,128]{1,0:T(8,128)}, f32[256,128]{1,0:T(8,128)}) custom-call(f32[128,128]{1,0:T(8,128)} %reshape.213.z_ref, f32[256,128]{1,0:T(8,128)} %bitcast.44, f32[256,128]{1,0:T(8,128)} %bitcast.51, f32[256,128]{1,0:T(8,128)} %bitcast.48, f32[256,128]{1,0:T(8,128)} %bitcast.49), custom_call_target="tpu_custom_call" | custom-call | tf_op jit(solution)/shard_map/kz_dft/pallas_call | solution.py:274
  99.9 5.0 %collective-permute-start.19 = (f32[2,16,8,128]{3,2,1,0:T(8,128)}, f32[2,16,8,128]{3,2,1,0:T(8,128)S(1)}, u32[]{:S(2)}, u32[]{:S(2)}) collective-permute-start(f32[2,16,8,128]{3,2,1,0:T(8,128)} %bitcast.55), channel_id=1, source_target_pairs={{0,1},{1,0},{2,3},{3,2},{4,5},{5,4},{6,7},{7,6},{8,9},{9,8},{10,11... | collective-permute-start | bytes 393224 | tf_op jit(solution)/shard_map/ppermute | solution.py:155
  105.7 1.6 %collective-permute-start.21 = (f32[2,16,8,128]{3,2,1,0:T(8,128)}, f32[2,16,8,128]{3,2,1,0:T(8,128)S(1)}, u32[]{:S(2)}, u32[]{:S(2)}) collective-permute-start(f32[2,16,8,128]{3,2,1,0:T(8,128)} %bitcast.53), channel_id=1, source_target_pairs={{0,3},{1,2},{2,1},{3,0},{4,7},{5,6},{6,5},{7,4},{8,11},{9,10},{10,... | collective-permute-start | bytes 393224 | tf_op jit(solution)/shard_map/ppermute | solution.py:155
  108.0 2.5 %kz_dft.2 = (f32[256,128]{1,0:T(8,128)}, f32[256,128]{1,0:T(8,128)}, f32[256,128]{1,0:T(8,128)}, f32[256,128]{1,0:T(8,128)}) custom-call(f32[128,128]{1,0:T(8,128)} %reshape.213.z_ref, f32[256,128]{1,0:T(8,128)} %bitcast.43, f32[256,128]{1,0:T(8,128)} %bitcast.52, f32[256,128]{1,0:T(8,128)} %bitcast.47, f32[256,128]{1,0:T(8,128)} %bitcast.50), custom_call_target="tpu_custom_call" | custom-call | tf_op jit(solution)/shard_map/kz_dft/pallas_call | solution.py:274
  110.6 2.2 %collective-permute-start.10 = (f32[2,16,8,128]{3,2,1,0:T(8,128)}, f32[2,16,8,128]{3,2,1,0:T(8,128)S(1)}, u32[]{:S(2)}, u32[]{:S(2)}) collective-permute-start(f32[2,16,8,128]{3,2,1,0:T(8,128)} %bitcast.58), channel_id=1, source_target_pairs={{0,3},{1,2},{2,1},{3,0},{4,7},{5,6},{6,5},{7,4},{8,11},{9,10},{10,... | collective-permute-start | bytes 393224 | tf_op jit(solution)/shard_map/ppermute | solution.py:155
  113.0 1.9 %collective-permute-start.9 = (f32[2,16,8,128]{3,2,1,0:T(8,128)}, f32[2,16,8,128]{3,2,1,0:T(8,128)S(1)}, u32[]{:S(2)}, u32[]{:S(2)}) collective-permute-start(f32[2,16,8,128]{3,2,1,0:T(8,128)} %bitcast.56), channel_id=1, source_target_pairs={{0,2},{1,3},{2,0},{3,1},{4,6},{5,7},{6,4},{7,5},{8,10},{9,11},{10,... | collective-permute-start | bytes 393224 | tf_op jit(solution)/shard_map/ppermute | solution.py:155
  115.0 5.8 %collective-permute-done.20.refs_6_ = f32[2,16,8,128]{3,2,1,0:T(8,128)S(1)} collective-permute-done((f32[2,16,8,128]{3,2,1,0:T(8,128)}, f32[2,16,8,128]{3,2,1,0:T(8,128)S(1)}, u32[]{:S(2)}, u32[]{:S(2)}) %collective-permute-start.20) | collective-permute-done | bytes 131104 | tf_op jit(solution)/shard_map/ppermute | solution.py:155
  121.6 7.9 %collective-permute-done.9.refs_2_ = f32[2,16,8,128]{3,2,1,0:T(8,128)S(1)} collective-permute-done((f32[2,16,8,128]{3,2,1,0:T(8,128)}, f32[2,16,8,128]{3,2,1,0:T(8,128)S(1)}, u32[]{:S(2)}, u32[]{:S(2)}) %collective-permute-start.9) | collective-permute-done | bytes 131104 | tf_op jit(solution)/shard_map/ppermute | solution.py:155
  130.1 2.4 %place.1 = f32[2,16,32,256]{3,2,1,0:T(8,128)} custom-call(s32[1]{0:T(128)} %bitcast.me_ref, f32[2,16,8,128]{3,2,1,0:T(8,128)} %bitcast.46, f32[2,16,8,128]{3,2,1,0:T(8,128)} %copy-done.12, f32[2,16,8,128]{3,2,1,0:T(8,128)} %copy-done.13, f32[2,16,8,128]{3,2,1,0:T(8,128)} %copy-done.11, f32[2,16,8,128]{3,2,1,0:T(8,128)} %bitcast.45, ...), custom_call_target="tpu_custom_call" | custom-call | tf_op jit(solution)/shard_map/place/pallas_call | solution.py:282
  (87 shorter events, 22.1 us)
Async XLA Ops:
  5.7 30.6 %copy-start.2 = (bf16[512,256]{1,0:T(8,128)(2,1)S(1)}, bf16[512,256]{1,0:T(8,128)(2,1)}, u32[]{:S(2)}) copy-start(bf16[512,256]{1,0:T(8,128)(2,1)} %constant.67.m2_ref) | copy-start | bytes 786436
  40.5 5.4 %collective-permute-start.11 = (f32[16,2,16,8,128]{4,3,2,1,0:T(8,128)S(1)}, f32[16,2,16,8,128]{4,3,2,1,0:T(8,128)S(1)}, u32[]{:S(2)}, u32[]{:S(2)}) collective-permute-start(f32[16,2,16,8,128]{4,3,2,1,0:T(8,128)S(1)} %get-tuple-element.28), channel_id=1, source_target_pairs={{0,4},{4,0},{8,12},{12,8},{16,20},{20,16},{24,28},{28,24},{1,5},{5... | collective-permute-start | bytes 6291464 | tf_op jit(solution)/shard_map/ppermute | solution.py:155
  45.1 5.8 %collective-permute-start = (f32[16,2,16,8,128]{4,3,2,1,0:T(8,128)S(1)}, f32[16,2,16,8,128]{4,3,2,1,0:T(8,128)S(1)}, u32[]{:S(2)}, u32[]{:S(2)}) collective-permute-start(f32[16,2,16,8,128]{4,3,2,1,0:T(8,128)S(1)} %get-tuple-element.22), channel_id=1, source_target_pairs={{0,4},{4,0},{8,12},{12,8},{16,20},{20,16},{24,28},{28,24},{1,5},{5... | collective-permute-start | bytes 6291464 | tf_op jit(solution)/shard_map/ppermute | solution.py:155
  46.3 15.8 %collective-permute-start.15 = (f32[4,2,16,8,128]{4,3,2,1,0:T(8,128)S(1)}, f32[4,2,16,8,128]{4,3,2,1,0:T(8,128)S(1)}, u32[]{:S(2)}, u32[]{:S(2)}) collective-permute-start(f32[4,2,16,8,128]{4,3,2,1,0:T(8,128)S(1)} %get-tuple-element.34), channel_id=1, source_target_pairs={{0,16},{4,20},{8,24},{12,28},{16,0},{20,4},{24,8},{28,12},{1,17},{... | collective-permute-start | bytes 1572872 | tf_op jit(solution)/shard_map/ppermute | solution.py:155
  49.4 14.9 %collective-permute-start.12 = (f32[4,2,16,8,128]{4,3,2,1,0:T(8,128)S(1)}, f32[4,2,16,8,128]{4,3,2,1,0:T(8,128)S(1)}, u32[]{:S(2)}, u32[]{:S(2)}) collective-permute-start(f32[4,2,16,8,128]{4,3,2,1,0:T(8,128)S(1)} %get-tuple-element.35), channel_id=1, source_target_pairs={{0,8},{4,12},{8,0},{12,4},{16,24},{20,28},{24,16},{28,20},{1,9},{5... | collective-permute-start | bytes 1572872 | tf_op jit(solution)/shard_map/ppermute | solution.py:155
  51.2 22.1 %collective-permute-start.4 = (f32[4,2,16,8,128]{4,3,2,1,0:T(8,128)S(1)}, f32[4,2,16,8,128]{4,3,2,1,0:T(8,128)S(1)}, u32[]{:S(2)}, u32[]{:S(2)}) collective-permute-start(f32[4,2,16,8,128]{4,3,2,1,0:T(8,128)S(1)} %get-tuple-element.38), channel_id=1, source_target_pairs={{0,16},{4,20},{8,24},{12,28},{16,0},{20,4},{24,8},{28,12},{1,17},{... | collective-permute-start | bytes 1572872 | tf_op jit(solution)/shard_map/ppermute | solution.py:155
  52.4 23.1 %collective-permute-start.1 = (f32[4,2,16,8,128]{4,3,2,1,0:T(8,128)S(1)}, f32[4,2,16,8,128]{4,3,2,1,0:T(8,128)S(1)}, u32[]{:S(2)}, u32[]{:S(2)}) collective-permute-start(f32[4,2,16,8,128]{4,3,2,1,0:T(8,128)S(1)} %get-tuple-element.39), channel_id=1, source_target_pairs={{0,8},{4,12},{8,0},{12,4},{16,24},{20,28},{24,16},{28,20},{1,9},{5... | collective-permute-start | bytes 1572872 | tf_op jit(solution)/shard_map/ppermute | solution.py:155
  62.1 18.9 %collective-permute-start.16 = (f32[2,2,16,8,128]{4,3,2,1,0:T(8,128)S(1)}, f32[2,2,16,8,128]{4,3,2,1,0:T(8,128)S(1)}, u32[]{:S(2)}, u32[]{:S(2)}) collective-permute-start(f32[2,2,16,8,128]{4,3,2,1,0:T(8,128)S(1)} %slice_add_fusion.8), channel_id=1, source_target_pairs={{0,8},{4,12},{8,0},{12,4},{16,24},{20,28},{24,16},{28,20},{1,9},{5... | collective-permute-start | bytes 786440 | tf_op jit(solution)/shard_map/ppermute | solution.py:155
  64.3 20.9 %collective-permute-start.13 = (f32[2,2,16,8,128]{4,3,2,1,0:T(8,128)S(1)}, f32[2,2,16,8,128]{4,3,2,1,0:T(8,128)S(1)}, u32[]{:S(2)}, u32[]{:S(2)}) collective-permute-start(f32[2,2,16,8,128]{4,3,2,1,0:T(8,128)S(1)} %slice_add_fusion.9), channel_id=1, source_target_pairs={{0,16},{4,20},{8,24},{12,28},{16,0},{20,4},{24,8},{28,12},{1,17},{... | collective-permute-start | bytes 786440 | tf_op jit(solution)/shard_map/ppermute | solution.py:155
  73.4 12.7 %collective-permute-start.5 = (f32[2,2,16,8,128]{4,3,2,1,0:T(8,128)S(1)}, f32[2,2,16,8,128]{4,3,2,1,0:T(8,128)S(1)}, u32[]{:S(2)}, u32[]{:S(2)}) collective-permute-start(f32[2,2,16,8,128]{4,3,2,1,0:T(8,128)S(1)} %slice_add_fusion.10), channel_id=1, source_target_pairs={{0,8},{4,12},{8,0},{12,4},{16,24},{20,28},{24,16},{28,20},{1,9},{5... | collective-permute-start | bytes 786440 | tf_op jit(solution)/shard_map/ppermute | solution.py:155
  75.5 13.5 %collective-permute-start.2 = (f32[2,2,16,8,128]{4,3,2,1,0:T(8,128)S(1)}, f32[2,2,16,8,128]{4,3,2,1,0:T(8,128)S(1)}, u32[]{:S(2)}, u32[]{:S(2)}) collective-permute-start(f32[2,2,16,8,128]{4,3,2,1,0:T(8,128)S(1)} %slice_add_fusion.11), channel_id=1, source_target_pairs={{0,16},{4,20},{8,24},{12,28},{16,0},{20,4},{24,8},{28,12},{1,17},{... | collective-permute-start | bytes 786440 | tf_op jit(solution)/shard_map/ppermute | solution.py:155
  81.1 14.0 %collective-permute-start.17 = (f32[2,16,8,128]{3,2,1,0:T(8,128)S(1)}, f32[2,16,8,128]{3,2,1,0:T(8,128)S(1)}, u32[]{:S(2)}, u32[]{:S(2)}) collective-permute-start(f32[2,16,8,128]{3,2,1,0:T(8,128)S(1)} %get-tuple-element.42), channel_id=1, source_target_pairs={{0,2},{1,3},{2,0},{3,1},{4,6},{5,7},{6,4},{7,5},{8,10},{9,11},{10,... | collective-permute-start | bytes 393224 | tf_op jit(solution)/shard_map/ppermute | solution.py:155
  83.8 12.9 %collective-permute-start.18 = (f32[2,16,8,128]{3,2,1,0:T(8,128)S(1)}, f32[2,16,8,128]{3,2,1,0:T(8,128)S(1)}, u32[]{:S(2)}, u32[]{:S(2)}) collective-permute-start(f32[2,16,8,128]{3,2,1,0:T(8,128)S(1)} %get-tuple-element.41), channel_id=1, source_target_pairs={{0,3},{1,2},{2,1},{3,0},{4,7},{5,6},{6,5},{7,4},{8,11},{9,10},{10,... | collective-permute-start | bytes 393224 | tf_op jit(solution)/shard_map/ppermute | solution.py:155
  85.9 10.8 %collective-permute-start.14 = (f32[2,16,8,128]{3,2,1,0:T(8,128)S(1)}, f32[2,16,8,128]{3,2,1,0:T(8,128)S(1)}, u32[]{:S(2)}, u32[]{:S(2)}) collective-permute-start(f32[2,16,8,128]{3,2,1,0:T(8,128)S(1)} %get-tuple-element.43), channel_id=1, source_target_pairs={{0,1},{1,0},{2,3},{3,2},{4,5},{5,4},{6,7},{7,6},{8,9},{9,8},{10,11... | collective-permute-start | bytes 393224 | tf_op jit(solution)/shard_map/ppermute | solution.py:155
  86.2 19.5 %collective-permute-start.6 = (f32[2,16,8,128]{3,2,1,0:T(8,128)S(1)}, f32[2,16,8,128]{3,2,1,0:T(8,128)S(1)}, u32[]{:S(2)}, u32[]{:S(2)}) collective-permute-start(f32[2,16,8,128]{3,2,1,0:T(8,128)S(1)} %get-tuple-element.46), channel_id=1, source_target_pairs={{0,2},{1,3},{2,0},{3,1},{4,6},{5,7},{6,4},{7,5},{8,10},{9,11},{10,... | collective-permute-start | bytes 393224 | tf_op jit(solution)/shard_map/ppermute | solution.py:155
  89.0 18.2 %collective-permute-start.7 = (f32[2,16,8,128]{3,2,1,0:T(8,128)S(1)}, f32[2,16,8,128]{3,2,1,0:T(8,128)S(1)}, u32[]{:S(2)}, u32[]{:S(2)}) collective-permute-start(f32[2,16,8,128]{3,2,1,0:T(8,128)S(1)} %get-tuple-element.45), channel_id=1, source_target_pairs={{0,3},{1,2},{2,1},{3,0},{4,7},{5,6},{6,5},{7,4},{8,11},{9,10},{10,... | collective-permute-start | bytes 393224 | tf_op jit(solution)/shard_map/ppermute | solution.py:155
  95.1 12.2 %collective-permute-start.3 = (f32[2,16,8,128]{3,2,1,0:T(8,128)S(1)}, f32[2,16,8,128]{3,2,1,0:T(8,128)S(1)}, u32[]{:S(2)}, u32[]{:S(2)}) collective-permute-start(f32[2,16,8,128]{3,2,1,0:T(8,128)S(1)} %get-tuple-element.47), channel_id=1, source_target_pairs={{0,1},{1,0},{2,3},{3,2},{4,5},{5,4},{6,7},{7,6},{8,9},{9,8},{10,11... | collective-permute-start | bytes 393224 | tf_op jit(solution)/shard_map/ppermute | solution.py:155
  99.9 13.1 %collective-permute-start.19 = (f32[2,16,8,128]{3,2,1,0:T(8,128)}, f32[2,16,8,128]{3,2,1,0:T(8,128)S(1)}, u32[]{:S(2)}, u32[]{:S(2)}) collective-permute-start(f32[2,16,8,128]{3,2,1,0:T(8,128)} %bitcast.55), channel_id=1, source_target_pairs={{0,1},{1,0},{2,3},{3,2},{4,5},{5,4},{6,7},{7,6},{8,9},{9,8},{10,11... | collective-permute-start | bytes 393224 | tf_op jit(solution)/shard_map/ppermute | solution.py:155
  104.9 15.9 %collective-permute-start.20 = (f32[2,16,8,128]{3,2,1,0:T(8,128)}, f32[2,16,8,128]{3,2,1,0:T(8,128)S(1)}, u32[]{:S(2)}, u32[]{:S(2)}) collective-permute-start(f32[2,16,8,128]{3,2,1,0:T(8,128)} %bitcast.54), channel_id=1, source_target_pairs={{0,2},{1,3},{2,0},{3,1},{4,6},{5,7},{6,4},{7,5},{8,10},{9,11},{10,... | collective-permute-start | bytes 393224 | tf_op jit(solution)/shard_map/ppermute | solution.py:155
  105.7 15.1 %collective-permute-start.21 = (f32[2,16,8,128]{3,2,1,0:T(8,128)}, f32[2,16,8,128]{3,2,1,0:T(8,128)S(1)}, u32[]{:S(2)}, u32[]{:S(2)}) collective-permute-start(f32[2,16,8,128]{3,2,1,0:T(8,128)} %bitcast.53), channel_id=1, source_target_pairs={{0,3},{1,2},{2,1},{3,0},{4,7},{5,6},{6,5},{7,4},{8,11},{9,10},{10,... | collective-permute-start | bytes 393224 | tf_op jit(solution)/shard_map/ppermute | solution.py:155
  110.6 10.2 %collective-permute-start.10 = (f32[2,16,8,128]{3,2,1,0:T(8,128)}, f32[2,16,8,128]{3,2,1,0:T(8,128)S(1)}, u32[]{:S(2)}, u32[]{:S(2)}) collective-permute-start(f32[2,16,8,128]{3,2,1,0:T(8,128)} %bitcast.58), channel_id=1, source_target_pairs={{0,3},{1,2},{2,1},{3,0},{4,7},{5,6},{6,5},{7,4},{8,11},{9,10},{10,... | collective-permute-start | bytes 393224 | tf_op jit(solution)/shard_map/ppermute | solution.py:155
  112.8 8.8 %collective-permute-start.8 = (f32[2,16,8,128]{3,2,1,0:T(8,128)}, f32[2,16,8,128]{3,2,1,0:T(8,128)S(1)}, u32[]{:S(2)}, u32[]{:S(2)}) collective-permute-start(f32[2,16,8,128]{3,2,1,0:T(8,128)} %bitcast.57), channel_id=1, source_target_pairs={{0,1},{1,0},{2,3},{3,2},{4,5},{5,4},{6,7},{7,6},{8,9},{9,8},{10,11... | collective-permute-start | bytes 393224 | tf_op jit(solution)/shard_map/ppermute | solution.py:155
  113.0 16.5 %copy-start.8 = (f32[2,16,8,128]{3,2,1,0:T(8,128)}, f32[2,16,8,128]{3,2,1,0:T(8,128)S(1)}, u32[]{:S(2)}) copy-start(f32[2,16,8,128]{3,2,1,0:T(8,128)S(1)} %collective-permute-done.19.refs_5_) | copy-start | bytes 393220
  113.0 16.5 %collective-permute-start.9 = (f32[2,16,8,128]{3,2,1,0:T(8,128)}, f32[2,16,8,128]{3,2,1,0:T(8,128)S(1)}, u32[]{:S(2)}, u32[]{:S(2)}) collective-permute-start(f32[2,16,8,128]{3,2,1,0:T(8,128)} %bitcast.56), channel_id=1, source_target_pairs={{0,2},{1,3},{2,0},{3,1},{4,6},{5,7},{6,4},{7,5},{8,10},{9,11},{10,... | collective-permute-start | bytes 393224 | tf_op jit(solution)/shard_map/ppermute | solution.py:155
  (18 other events, 51.4 us)
